TPU v7x, 32 devices: a whole 2x2x4 slice. The times are simulated.
32 devices in a mesh: py: 4 (over z), pz: 8 (over y, x, core).
Axes of the slice: x: 2, y: 2, z: 4, core: 2. Of those that a mesh axis runs over, the one named last changes fastest.
Arguments:
- field: bfloat16 [128, 128, 64, 256], P('py', 'pz'), may hold values from -60 to 60
- spectral_weights: bfloat16 [32, 32, 32, 2, 64, 64], P('py', 'pz'), may hold values from -0.5 to 0.5
- bypass_weight: bfloat16 [64, 64], replicated, may hold values from -0.75 to 0.75
Outputs:
- normalized: bfloat16 [128, 128, 64, 256], P('py', 'pz')
All inputs are finite; a program needn't handle non-finite values.
Results may differ from a plain program's by a relative error of at most 0.0081.
Values may be sent and summed in bfloat16 or wider, within the bound.
A program may use at most 192 MiB of HBM per device.

v0:
```python
import math
import jax
import jax.numpy as jnp
from jax import lax
from jax.sharding import PartitionSpec as P

NX = 256
NY = 128
NZ = 128
C = 64
MODES = 32


def mode_frequencies(mode_count):
    ordinal = jnp.arange(mode_count, dtype=jnp.float32)
    return jnp.where(ordinal < mode_count // 2, ordinal, ordinal - mode_count)


def phase_angles(length, mode_count):
    points = jnp.arange(length, dtype=jnp.float32)
    return 2.0 * math.pi / length * points[:, None] * mode_frequencies(mode_count)[None, :]


def real_forward(length, mode_count):
    angles = phase_angles(length, mode_count)
    matrix = jnp.stack([jnp.cos(angles), -jnp.sin(angles)], axis=2).reshape(length, 2 * mode_count)
    return (matrix / math.sqrt(length)).astype(jnp.bfloat16)


def complex_forward(length, mode_count):
    angles = phase_angles(length, mode_count)
    cosine = jnp.cos(angles)
    sine_part = jnp.sin(angles)
    from_real = jnp.stack([cosine, -sine_part], axis=2)
    from_imag = jnp.stack([sine_part, cosine], axis=2)
    return (jnp.stack([from_real, from_imag], axis=1) / math.sqrt(length)).astype(jnp.bfloat16)


def complex_inverse(length, mode_count):
    angles = phase_angles(length, mode_count).T
    cosine = jnp.cos(angles)
    sine_part = jnp.sin(angles)
    from_real = jnp.stack([cosine, sine_part], axis=2)
    from_imag = jnp.stack([-sine_part, cosine], axis=2)
    return (jnp.stack([from_real, from_imag], axis=1) / math.sqrt(mode_count)).astype(jnp.bfloat16)


def real_inverse(length, mode_count):
    angles = phase_angles(length, mode_count).T
    matrix = jnp.stack([jnp.cos(angles), -jnp.sin(angles)], axis=1).reshape(2 * mode_count, length)
    return (matrix / math.sqrt(mode_count)).astype(jnp.bfloat16)


def mix_modes(spectrum, weights):
    real_in = spectrum[..., 0]
    imag_in = spectrum[..., 1]
    real_w = weights[:, :, :, 0]
    imag_w = weights[:, :, :, 1]

    def product(operand, coefficient):
        return jnp.einsum(
            "cabk,abkco->oabk", operand, coefficient, preferred_element_type=jnp.float32
        )

    real_out = product(real_in, real_w) - product(imag_in, imag_w)
    imag_out = product(real_in, imag_w) + product(imag_in, real_w)
    return jnp.stack([real_out, imag_out], axis=-1).astype(jnp.bfloat16)


def on_device(field, spectral_weights, bypass_weight):
    row_table = real_forward(NX, MODES)
    forward_plane = complex_forward(NY, MODES)
    forward_column = complex_forward(NZ, MODES)
    inverse_column = complex_inverse(NZ, MODES)
    inverse_plane = complex_inverse(NY, MODES)
    inverse_row = real_inverse(NX, MODES)
    flat = jnp.dot(field.reshape(-1, NX), row_table, preferred_element_type=jnp.float32)
    row_modes = flat.reshape(field.shape[:3] + (2 * MODES,)).astype(jnp.bfloat16)
    incoming = lax.all_to_all(row_modes, "py", split_axis=3, concat_axis=0, tiled=True)
    paired = incoming.reshape(incoming.shape[:3] + (-1, 2))
    plane_modes = jnp.einsum(
        "yzcmp,ypkq->zcmkq", paired, forward_plane, preferred_element_type=jnp.float32
    ).astype(jnp.bfloat16)
    plane_modes = plane_modes.reshape(plane_modes.shape[:3] + (-1,))
    incoming = lax.all_to_all(plane_modes, "pz", split_axis=3, concat_axis=0, tiled=True)
    paired = incoming.reshape(incoming.shape[:3] + (-1, 2))
    spectrum = jnp.einsum(
        "zcakp,zpjq->cakjq", paired, forward_column, preferred_element_type=jnp.float32
    ).astype(jnp.bfloat16)
    mixed_modes = mix_modes(spectrum, spectral_weights)
    column_back = jnp.einsum(
        "oabkp,kpzq->zoabq", mixed_modes, inverse_column, preferred_element_type=jnp.float32
    ).astype(jnp.bfloat16)
    column_back = column_back.reshape(column_back.shape[:3] + (-1,))
    incoming = lax.all_to_all(column_back, "pz", split_axis=0, concat_axis=3, tiled=True)
    paired = incoming.reshape(incoming.shape[:3] + (-1, 2))
    plane_back = jnp.einsum(
        "zcakp,kpyq->yzcaq", paired, inverse_plane, preferred_element_type=jnp.float32
    ).astype(jnp.bfloat16)
    plane_back = plane_back.reshape(plane_back.shape[:3] + (-1,))
    incoming = lax.all_to_all(plane_back, "py", split_axis=0, concat_axis=3, tiled=True)
    points = jnp.dot(
        incoming.reshape(-1, 2 * MODES), inverse_row, preferred_element_type=jnp.float32
    )
    spectral = points.reshape(incoming.shape[:3] + (NX,))
    bypass = jnp.einsum("yzcx,co->yzox", field, bypass_weight, preferred_element_type=jnp.float32)
    activated = jax.nn.gelu(spectral + bypass, approximate=True)
    entries = NX * NY * NZ * C
    summed, squared = lax.psum((jnp.sum(activated), jnp.sum(activated * activated)), ("py", "pz"))
    field_mean = summed / entries
    field_var = squared / entries - field_mean * field_mean
    return ((activated - field_mean) * lax.rsqrt(field_var + 1e-05)).astype(jnp.bfloat16)


def solution(mesh):
    in_specs = (P("py", "pz", None, None), P("py", "pz", None, None, None, None), P())
    out_specs = P("py", "pz", None, None)
    return jax.shard_map(
        on_device, mesh=mesh, in_specs=in_specs, out_specs=out_specs, check_vma=False
    )
```

profile of v0, /device:TPU:12, one launch (start us, length us, event | category | flops | bytes accessed | tf_op | source)
XLA Modules:
  0.0 524.4 jit_solution(14442338689824171746)
XLA Ops:
  0.3 12.8 %fusion = bf16[32768,64]{0,1:T(8,128)(2,1)} fusion(bf16[256,64]{0,1:T(8,128)(2,1)S(1)} %convert_element_type.65, bf16[32768,256]{1,0:T(8,128)(2,1)} %bitcast.144), kind=kOutput, calls=%fused_computation.2 | convolution fusion | flops 1075838976 | bytes 21004288 | tf_op jit(solution)/shard_map/dot_general | solution.py:77
  13.2 11.3 %convert_element_type.68 = bf16[32,16,64,64]{2,1,0,3:T(8,128)(2,1)} reshape(bf16[32768,64]{0,1:T(8,128)(2,1)} %fusion) | data formatting | bytes 8388608 | tf_op jit(solution)/shard_map/convert_element_type | solution.py:78
  24.5 9.5 %reshape.532 = bf16[4,2,262144]{2,1,0:T(2,128)(2,1)} reshape(bf16[64,32,16,64]{3,2,1,0:T(8,128)(2,1)} %bitcast.145) | data formatting | bytes 8388608
  34.0 5.8 %all-to-all-start = ((bf16[4,2,262144]{2,1,0:T(2,128)(2,1)}), bf16[4,2,262144]{2,1,0:T(2,128)(2,1)}, u32[]{:S(2)}, u32[]{:S(2)}) async-start(bf16[4,2,262144]{2,1,0:T(2,128)(2,1)} %reshape.532), calls=%async_computation | async-start | bytes 8388608 | tf_op jit(solution)/shard_map/all_to_all | solution.py:79
  40.0 89.9 %all-to-all-done = bf16[4,2,262144]{2,1,0:T(2,128)(2,1)} async-done(((bf16[4,2,262144]{2,1,0:T(2,128)(2,1)}), bf16[4,2,262144]{2,1,0:T(2,128)(2,1)}, u32[]{:S(2)}, u32[]{:S(2)}) %all-to-all-start) | async-done | bytes 4194336 | tf_op jit(solution)/shard_map/all_to_all | solution.py:79
  129.9 9.3 %reshape.533 = bf16[64,32,16,64]{3,2,1,0:T(8,128)(2,1)} reshape(bf16[4,2,262144]{2,1,0:T(2,128)(2,1)} %all-to-all-done) | data formatting | bytes 8388608
  139.1 9.0 %copy.102 = bf16[4,32,16,64,16]{3,2,4,1,0:T(8,128)(2,1)} copy(bf16[4,32,16,64,16]{3,2,1,4,0:T(8,128)(2,1)} %bitcast.147) | data formatting | bytes 8388608 | tf_op jit(solution)/shard_map/all_to_all | solution.py:79
  148.2 13.8 %copy.120 = bf16[128,16,64,8,2,1]{0,3,4,5,2,1:T(8,128)(2,1)} copy(bf16[128,16,64,8,2,1]{2,1,4,3,0,5:T(8,128)(2,1)} %bitcast.148) | data formatting | bytes 8388608 | tf_op jit(solution)/shard_map/reshape | solution.py:80
  161.9 5.4 %bitcast_convert_fusion.1 = bf16[16,64,8,32,2]{3,2,4,1,0:T(8,128)(2,1)} fusion(bf16[128,16,64,8,2,1]{0,3,4,5,2,1:T(8,128)(2,1)} %copy.120, f32[128,1,32,2]{0,2,1,3:T(8,128)S(1)} %get-tuple-element.14, f32[128,1,32,2]{0,2,1,3:T(8,128)S(1)} %get-tuple-element.13), kind=kOutput, calls=%fused_computation.26 | convolution fusion | flops 269008896 | bytes 5308416 | tf_op jit(solution)/shard_map/yzcmp,ypkq->zcmkq/dot_general | solution.py:81
  167.3 6.0 %copy.140 = bf16[16,64,8,32,2]{1,2,0,4,3:T(8,128)(2,1)S(1)} copy(bf16[16,64,8,32,2]{3,2,4,1,0:T(8,128)(2,1)} %bitcast_convert_fusion.1) | data formatting | bytes 2097152 | tf_op jit(solution)/shard_map/reshape | solution.py:84
  173.4 2.7 reshape.534
  176.0 4.4 all-to-all-start.1
  180.6 13.7 %all-to-all-done.1 = bf16[8,2,32768]{2,1,0:T(2,128)(2,1)S(1)} async-done(((bf16[8,2,32768]{2,1,0:T(2,128)(2,1)}), bf16[8,2,32768]{2,1,0:T(2,128)(2,1)S(1)}, u32[]{:S(2)}, u32[]{:S(2)}) %all-to-all-start.1) | async-done | bytes 1048608 | tf_op jit(solution)/shard_map/all_to_all | solution.py:85
  197.7 4.5 copy.123
  203.5 8.1 %fusion.8 = f32[8,4,32,1,64]{4,3,2,1,0:T(1,128)S(1)} fusion(bf16[64,8,4,32,1]{0,4,3,2,1:T(2,128)(2,1)S(1)} %copy.125, bf16[8,4,32,2,64,64]{5,4,3,2,1,0:T(8,128)(2,1)} %param.4), kind=kOutput, calls=%fused_computation.13 | convolution fusion | flops 8388608 | bytes 17170432 | tf_op jit(solution)/shard_map/cabk,abkco->oabk/dot_general | solution.py:61
  211.6 8.1 %fusion.14 = f32[8,4,32,1,64]{4,3,2,1,0:T(1,128)S(1)} fusion(bf16[64,8,4,32,1]{0,4,3,2,1:T(2,128)(2,1)S(1)} %copy.125, bf16[8,4,32,2,64,64]{5,4,3,2,1,0:T(8,128)(2,1)} %param.4), kind=kOutput, calls=%fused_computation.19 | convolution fusion | flops 8388608 | bytes 17170432 | tf_op jit(solution)/shard_map/cabk,abkco->oabk/dot_general | solution.py:61
  220.4 8.1 %fusion.12 = f32[8,4,32,1,64]{4,3,2,1,0:T(1,128)S(1)} fusion(bf16[64,8,4,32,1]{0,4,3,2,1:T(2,128)(2,1)S(1)} %copy.127, bf16[8,4,32,2,64,64]{5,4,3,2,1,0:T(8,128)(2,1)} %param.4), kind=kOutput, calls=%fused_computation.17 | convolution fusion | flops 8388608 | bytes 17170432 | tf_op jit(solution)/shard_map/cabk,abkco->oabk/dot_general | solution.py:61
  228.5 8.3 %fusion.10 = f32[8,4,32,1,64]{4,3,2,1,0:T(1,128)S(1)} fusion(bf16[64,8,4,32,1]{0,4,3,2,1:T(2,128)(2,1)S(1)} %copy.127, bf16[8,4,32,2,64,64]{5,4,3,2,1,0:T(8,128)(2,1)} %param.4), kind=kOutput, calls=%fused_computation.15 | convolution fusion | flops 8388608 | bytes 17170432 | tf_op jit(solution)/shard_map/cabk,abkco->oabk/dot_general | solution.py:61
  238.2 3.5 copy.111
  243.4 18.4 %all_to_all.60 = bf16[8,2,32768]{2,1,0:T(2,128)(2,1)} all-to-all(bf16[8,2,32768]{2,1,0:T(2,128)(2,1)S(1)} %reshape.536), channel_id=1, replica_groups=mesh['py'=4,'pz'=8] {'pz'}, dimensions={0} | all-to-all | bytes 2097152 | tf_op jit(solution)/shard_map/all_to_all | solution.py:95
  261.8 3.1 reshape.537
  266.9 2.9 copy.114
  269.8 12.8 %copy.115 = bf16[128,16,64,16]{2,3,1,0:T(8,128)(2,1)} copy(bf16[128,16,64,16]{0,2,3,1:T(8,128)(2,1)} %bitcast.150) | data formatting | bytes 8388608 | tf_op jit(solution)/shard_map/reshape | solution.py:100
  282.6 9.5 %reshape.538 = bf16[4,2,262144]{2,1,0:T(2,128)(2,1)} reshape(bf16[128,16,16,64]{3,2,1,0:T(8,128)(2,1)} %bitcast.146) | data formatting | bytes 8388608
  292.2 8.4 %all-to-all-start.3 = ((bf16[4,2,262144]{2,1,0:T(2,128)(2,1)}), bf16[4,2,262144]{2,1,0:T(2,128)(2,1)}, u32[]{:S(2)}, u32[]{:S(2)}) async-start(bf16[4,2,262144]{2,1,0:T(2,128)(2,1)} %reshape.538), calls=%async_computation.3 | async-start | bytes 8388608 | tf_op jit(solution)/shard_map/all_to_all | solution.py:101
  300.9 89.3 %all-to-all-done.3 = bf16[4,2,262144]{2,1,0:T(2,128)(2,1)} async-done(((bf16[4,2,262144]{2,1,0:T(2,128)(2,1)}), bf16[4,2,262144]{2,1,0:T(2,128)(2,1)}, u32[]{:S(2)}, u32[]{:S(2)}) %all-to-all-start.3) | async-done | bytes 4194336 | tf_op jit(solution)/shard_map/all_to_all | solution.py:101
  390.2 9.3 %reshape.539 = bf16[128,16,16,64]{3,2,1,0:T(8,128)(2,1)} reshape(bf16[4,2,262144]{2,1,0:T(2,128)(2,1)} %all-to-all-done.3) | data formatting | bytes 8388608
  399.4 9.0 %copy.116 = bf16[32,16,64,4,16]{2,4,3,1,0:T(8,128)(2,1)} copy(bf16[32,16,64,4,16]{2,4,1,0,3:T(8,128)(2,1)} %bitcast.149) | data formatting | bytes 8388608 | tf_op jit(solution)/shard_map/all_to_all | solution.py:101
  408.5 19.0 %fusion.36 = f32[32,16,64,256]{3,2,1,0:T(8,128)} fusion(bf16[32,16,64,64]{2,3,1,0:T(8,128)(2,1)} %bitcast.143, bf16[64,256,1,1]{1,0,2,3:T(8,128)(2,1)S(1)} %reshape.529), kind=kOutput, calls=%fused_computation.62 | convolution fusion | flops 1073741824 | bytes 37781504 | tf_op jit(solution)/shard_map/dot_general | solution.py:102
  427.5 32.3 %fusion.54 = (f32[]{:T(128)}, f32[]{:T(128)}, f32[32,16,64,256]{3,2,1,0:T(8,128)}) fusion(f32[32,16,64,256]{3,2,1,0:T(8,128)} %fusion.36, bf16[32,16,64,256]{3,2,1,0:T(8,128)(2,1)} %param.3, bf16[64,64]{1,0:T(8,128)(2,1)S(1)} %copy-done), kind=kOutput, calls=%fused_computation.83 | convolution fusion | flops 1174405120 | bytes 83894280 | tf_op jit(solution)/shard_map/yzcx,co->yzox/dot_general | solution.py:106
  459.8 43.2 %all-reduce = (f32[]{:T(128)}, f32[]{:T(128)}) all-reduce(f32[]{:T(128)} %get-tuple-element.6, f32[]{:T(128)} %get-tuple-element.5), channel_id=1, replica_groups=mesh['py'=4,'pz'=8] {'py','pz'}, use_global_device_ids=true, to_apply=%region_3.4 | all-reduce | flops 2 | bytes 16 | tf_op jit(solution)/shard_map/psum | solution.py:109
  505.5 18.5 %multiply_convert_fusion = bf16[32,16,64,256]{3,2,1,0:T(8,128)(2,1)} fusion(f32[32,16,64,256]{3,2,1,0:T(8,128)} %get-tuple-element.25, f32[]{:T(128)S(6)} %rsqrt.3, f32[]{:T(128)S(6)} %div.32), kind=kLoop, calls=%fused_computation.11 | loop fusion | flops 25165824 | bytes 50331656 | tf_op jit(solution)/shard_map/convert_element_type | solution.py:112
  (29 shorter events, 11.2 us)
Async XLA Ops:
  0.0 427.5 %copy-start = (bf16[64,64]{1,0:T(8,128)(2,1)S(1)}, bf16[64,64]{1,0:T(8,128)(2,1)}, u32[]{:S(2)}) copy-start(bf16[64,64]{1,0:T(8,128)(2,1)} %param.5) | copy-start | bytes 24580
  34.0 95.8 %all-to-all-start = ((bf16[4,2,262144]{2,1,0:T(2,128)(2,1)}), bf16[4,2,262144]{2,1,0:T(2,128)(2,1)}, u32[]{:S(2)}, u32[]{:S(2)}) async-start(bf16[4,2,262144]{2,1,0:T(2,128)(2,1)} %reshape.532), calls=%async_computation | async-start | bytes 8388608 | tf_op jit(solution)/shard_map/all_to_all | solution.py:79
  176.0 18.3 %all-to-all-start.1 = ((bf16[8,2,32768]{2,1,0:T(2,128)(2,1)}), bf16[8,2,32768]{2,1,0:T(2,128)(2,1)S(1)}, u32[]{:S(2)}, u32[]{:S(2)}) async-start(bf16[8,2,32768]{2,1,0:T(2,128)(2,1)} %reshape.534), calls=%async_computation.1 | async-start | bytes 2097152 | tf_op jit(solution)/shard_map/all_to_all | solution.py:85
  292.2 98.0 %all-to-all-start.3 = ((bf16[4,2,262144]{2,1,0:T(2,128)(2,1)}), bf16[4,2,262144]{2,1,0:T(2,128)(2,1)}, u32[]{:S(2)}, u32[]{:S(2)}) async-start(bf16[4,2,262144]{2,1,0:T(2,128)(2,1)} %reshape.538), calls=%async_computation.3 | async-start | bytes 8388608 | tf_op jit(solution)/shard_map/all_to_all | solution.py:101
where the time goes:
time: 531 us; the launch traced here: 524 us
  waiting for transfers between devices  193 us (36%)
  local copies, waits for them, and re-layouts  124 us (23%)
  matrix products  104 us (20%)
  blocking collectives  61.6 us (12%)
  other arithmetic  19.5 us (4%)
  starting transfers between devices  18.7 us (4%)
    all_to_all x1, waiting for transfers between devices, on_device(): lax.all_to_all(row_modes, 'py', split_axis=3, concat_axis=0, tiled=True)  89.9 us
    all_to_all x1, waiting for transfers between devices, on_device(): lax.all_to_all(plane_back, 'py', split_axis=0, concat_axis=3, tiled=True)  89.3 us
    unnamed x10, local copies, waits for them, and re-layouts  46.5 us
    psum x1, blocking collectives, on_device(): lax.psum((jnp.sum(activated), jnp.sum(activated * activated)), ('py', 'pz'))  43.2 us
    dot_general x4, matrix products, product(): jnp.einsum('cabk,abkco->oabk', operand, coefficient, preferred_element_ty...  32.6 us
    dot_general x1, matrix products, on_device(): jnp.einsum('yzcx,co->yzox', field, bypass_weight, preferred_element_type=...  32.3 us
    dot_general x1, matrix products, on_device(): jnp.dot(incoming.reshape(-1, 2 * MODES), inverse_row, preferred_element_t...  19 us
    convert_element_type x1, other arithmetic, on_device(): ((activated - field_mean) * lax.rsqrt(field_var + 1e-05)).astype(jnp.bflo...  18.5 us
  transfers between devices with their start and end apart: 3, of which 3 were waited for; matrix products, arithmetic and copies ran while one was open for 0% of the time, Pallas kernels for 0%

commit v1 on v0

--- a/solution.py
+++ b/solution.py
@@ -98,7 +98,12 @@
         "zcakp,kpyq->yzcaq", paired, inverse_plane, preferred_element_type=jnp.float32
     ).astype(jnp.bfloat16)
     plane_back = plane_back.reshape(plane_back.shape[:3] + (-1,))
-    incoming = lax.all_to_all(plane_back, "py", split_axis=0, concat_axis=3, tiled=True)
+    incoming = jnp.concatenate(
+        jax.lax.all_to_all(
+            jnp.stack(jnp.split(plane_back, jax.lax.psum(1, "py"), axis=0)), "py", 0, 0
+        ),
+        axis=3,
+    )
     points = jnp.dot(
         incoming.reshape(-1, 2 * MODES), inverse_row, preferred_element_type=jnp.float32
     )

time: 531 us -> 563 us (1.060)
  local copies, waits for them, and re-layouts: 124 us -> 149 us
  other arithmetic: 19.5 us -> 26.7 us
    split x0 -> x5, local copies, waits for them, and re-layouts: none -> 31.3 us  [on_device(): jnp.split(plane_back, jax.lax.psum(1, 'py'), axis=0)]
    all_to_all x1 -> x0, local copies, waits for them, and re-layouts: 9.03 us -> none  [on_device(): lax.all_to_all(plane_back, 'py', split_axis=0, concat_axis=3, tiled=True)]
    unnamed x0 -> x1, other arithmetic: none -> 7.2 us
    reshape x1 -> x2, local copies, waits for them, and re-layouts: 12.8 us -> 18.7 us  [on_device(): jnp.concatenate(jax.lax.all_to_all(jnp.stack(jnp.split(plane_back, jax.la...]
where the time goes in v1:
time: 563 us; the launch traced here: 557 us
  waiting for transfers between devices  193 us (34%)
  local copies, waits for them, and re-layouts  149 us (26%)
  matrix products  105 us (19%)
  blocking collectives  61.6 us (11%)
  other arithmetic  26.7 us (5%)
  starting transfers between devices  18.3 us (3%)
    all_to_all x1, waiting for transfers between devices, on_device(): lax.all_to_all(row_modes, 'py', split_axis=3, concat_axis=0, tiled=True)  89.9 us
    all_to_all x1, waiting for transfers between devices, on_device(): jax.lax.all_to_all(jnp.stack(jnp.split(plane_back, jax.lax.psum(1, 'py'),...  89.3 us
    unnamed x10, local copies, waits for them, and re-layouts  46.5 us
    psum x1, blocking collectives, on_device(): lax.psum((jnp.sum(activated), jnp.sum(activated * activated)), ('py', 'pz'))  43.2 us
    dot_general x4, matrix products, product(): jnp.einsum('cabk,abkco->oabk', operand, coefficient, preferred_element_ty...  32.8 us
    dot_general x1, matrix products, on_device(): jnp.einsum('yzcx,co->yzox', field, bypass_weight, preferred_element_type=...  32.5 us
    split x5, local copies, waits for them, and re-layouts, on_device(): jnp.split(plane_back, jax.lax.psum(1, 'py'), axis=0)  31.3 us
    dot_general x1, matrix products, on_device(): jnp.dot(incoming.reshape(-1, 2 * MODES), inverse_row, preferred_element_t...  19 us
  transfers between devices with their start and end apart: 3, of which 3 were waited for; matrix products, arithmetic and copies ran while one was open for 0% of the time, Pallas kernels for 0%

profile of v1, /device:TPU:12, one launch (start us, length us, event | category | flops | bytes accessed | tf_op | source)
XLA Modules:
  0.0 556.8 jit_solution(14066024160221188082)
XLA Ops:
  0.3 12.9 %fusion = bf16[32768,64]{0,1:T(8,128)(2,1)} fusion(bf16[256,64]{0,1:T(8,128)(2,1)S(1)} %convert_element_type.65, bf16[32768,256]{1,0:T(8,128)(2,1)} %bitcast.148), kind=kOutput, calls=%fused_computation.2 | convolution fusion | flops 1075838976 | bytes 21004288 | tf_op jit(solution)/shard_map/dot_general | solution.py:77
  13.2 11.3 %convert_element_type.68 = bf16[32,16,64,64]{2,1,0,3:T(8,128)(2,1)} reshape(bf16[32768,64]{0,1:T(8,128)(2,1)} %fusion) | data formatting | bytes 8388608 | tf_op jit(solution)/shard_map/convert_element_type | solution.py:78
  24.5 9.5 %reshape.539 = bf16[4,2,262144]{2,1,0:T(2,128)(2,1)} reshape(bf16[64,32,16,64]{3,2,1,0:T(8,128)(2,1)} %bitcast.149) | data formatting | bytes 8388608
  34.0 5.5 all-to-all-start
  39.7 89.9 %all-to-all-done = bf16[4,2,262144]{2,1,0:T(2,128)(2,1)} async-done(((bf16[4,2,262144]{2,1,0:T(2,128)(2,1)}), bf16[4,2,262144]{2,1,0:T(2,128)(2,1)}, u32[]{:S(2)}, u32[]{:S(2)}) %all-to-all-start) | async-done | bytes 4194336 | tf_op jit(solution)/shard_map/all_to_all | solution.py:79
  129.6 9.3 %reshape.540 = bf16[64,32,16,64]{3,2,1,0:T(8,128)(2,1)} reshape(bf16[4,2,262144]{2,1,0:T(2,128)(2,1)} %all-to-all-done) | data formatting | bytes 8388608
  138.8 9.0 %copy.112 = bf16[4,32,16,64,16]{3,2,4,1,0:T(8,128)(2,1)} copy(bf16[4,32,16,64,16]{3,2,1,4,0:T(8,128)(2,1)} %bitcast.150) | data formatting | bytes 8388608 | tf_op jit(solution)/shard_map/all_to_all | solution.py:79
  147.9 13.8 %copy.132 = bf16[128,16,64,8,2,1]{0,3,4,5,2,1:T(8,128)(2,1)} copy(bf16[128,16,64,8,2,1]{2,1,4,3,0,5:T(8,128)(2,1)} %bitcast.151) | data formatting | bytes 8388608 | tf_op jit(solution)/shard_map/reshape | solution.py:80
  161.6 5.4 bitcast_convert_fusion.1
  167.0 6.0 %copy.152 = bf16[16,64,8,32,2]{1,2,0,4,3:T(8,128)(2,1)S(1)} copy(bf16[16,64,8,32,2]{3,2,4,1,0:T(8,128)(2,1)} %bitcast_convert_fusion.1) | data formatting | bytes 2097152 | tf_op jit(solution)/shard_map/reshape | solution.py:84
  180.4 13.7 %all-to-all-done.1 = bf16[8,2,32768]{2,1,0:T(2,128)(2,1)S(1)} async-done(((bf16[8,2,32768]{2,1,0:T(2,128)(2,1)}), bf16[8,2,32768]{2,1,0:T(2,128)(2,1)S(1)}, u32[]{:S(2)}, u32[]{:S(2)}) %all-to-all-start.1) | async-done | bytes 1048608 | tf_op jit(solution)/shard_map/all_to_all | solution.py:85
  203.2 8.1 %fusion.8 = f32[8,4,32,1,64]{4,3,2,1,0:T(1,128)S(1)} fusion(bf16[64,8,4,32,1]{0,4,3,2,1:T(2,128)(2,1)S(1)} %copy.137, bf16[8,4,32,2,64,64]{5,4,3,2,1,0:T(8,128)(2,1)} %param.4), kind=kOutput, calls=%fused_computation.13 | convolution fusion | flops 8388608 | bytes 17170432 | tf_op jit(solution)/shard_map/cabk,abkco->oabk/dot_general | solution.py:61
  211.3 8.1 %fusion.14 = f32[8,4,32,1,64]{4,3,2,1,0:T(1,128)S(1)} fusion(bf16[64,8,4,32,1]{0,4,3,2,1:T(2,128)(2,1)S(1)} %copy.137, bf16[8,4,32,2,64,64]{5,4,3,2,1,0:T(8,128)(2,1)} %param.4), kind=kOutput, calls=%fused_computation.19 | convolution fusion | flops 8388608 | bytes 17170432 | tf_op jit(solution)/shard_map/cabk,abkco->oabk/dot_general | solution.py:61
  220.1 8.1 %fusion.12 = f32[8,4,32,1,64]{4,3,2,1,0:T(1,128)S(1)} fusion(bf16[64,8,4,32,1]{0,4,3,2,1:T(2,128)(2,1)S(1)} %copy.139, bf16[8,4,32,2,64,64]{5,4,3,2,1,0:T(8,128)(2,1)} %param.4), kind=kOutput, calls=%fused_computation.17 | convolution fusion | flops 8388608 | bytes 17170432 | tf_op jit(solution)/shard_map/cabk,abkco->oabk/dot_general | solution.py:61
  228.2 8.5 %fusion.10 = f32[8,4,32,1,64]{4,3,2,1,0:T(1,128)S(1)} fusion(bf16[64,8,4,32,1]{0,4,3,2,1:T(2,128)(2,1)S(1)} %copy.139, bf16[8,4,32,2,64,64]{5,4,3,2,1,0:T(8,128)(2,1)} %param.4), kind=kOutput, calls=%fused_computation.15 | convolution fusion | flops 8388608 | bytes 17170432 | tf_op jit(solution)/shard_map/cabk,abkco->oabk/dot_general | solution.py:61
  243.3 18.4 %all_to_all.50 = bf16[8,2,32768]{2,1,0:T(2,128)(2,1)} all-to-all(bf16[8,2,32768]{2,1,0:T(2,128)(2,1)S(1)} %reshape.543), channel_id=1, replica_groups=mesh['py'=4,'pz'=8] {'pz'}, dimensions={0} | all-to-all | bytes 2097152 | tf_op jit(solution)/shard_map/all_to_all | solution.py:95
  266.8 7.8 %fusion.55 = (bf16[32,16,64,8,2]{0,2,3,1,4:T(8,128)(2,1)}, bf16[32,16,64,8,2]{0,2,3,1,4:T(8,128)(2,1)}, bf16[32,16,64,8,2]{0,2,3,1,4:T(8,128)(2,1)}, bf16[32,16,64,8,2]{0,2,3,1,4:T(8,128)(2,1)}) fusion(bf16[128,16,64,8,2]{0,2,3,1,4:T(8,128)(2,1)S(1)} %fusion.20), kind=kLoop, calls=%fused_computation.85 | loop fusion | bytes 8388608 | tf_op jit(solution)/shard_map/split | solution.py:103
  274.7 5.2 copy.124
  279.8 6.1 %copy.127 = bf16[32,16,64,8,2]{2,1,4,3,0:T(8,128)(2,1)} copy(bf16[32,16,64,8,2]{0,2,3,1,4:T(8,128)(2,1)} %get-tuple-element.10) | data formatting | bytes 2097152 | tf_op jit(solution)/shard_map/split | solution.py:103
  285.9 6.1 %copy.126 = bf16[32,16,64,8,2]{2,1,4,3,0:T(8,128)(2,1)} copy(bf16[32,16,64,8,2]{0,2,3,1,4:T(8,128)(2,1)} %get-tuple-element.11) | data formatting | bytes 2097152 | tf_op jit(solution)/shard_map/split | solution.py:103
  292.0 6.1 %copy.125 = bf16[32,16,64,8,2]{2,1,4,3,0:T(8,128)(2,1)} copy(bf16[32,16,64,8,2]{0,2,3,1,4:T(8,128)(2,1)} %get-tuple-element.12) | data formatting | bytes 2097152 | tf_op jit(solution)/shard_map/split | solution.py:103
  298.1 7.2 %fusion.56 = bf16[4,32,16,16,64]{4,3,2,1,0:T(8,128)(2,1)} fusion(bf16[1,32,16,64,16]{3,2,4,1,0:T(8,128)(2,1)} %bitcast.159, bf16[1,32,16,64,16]{3,2,4,1,0:T(8,128)(2,1)} %bitcast.160, bf16[1,32,16,64,16]{3,2,4,1,0:T(8,128)(2,1)} %bitcast.161, bf16[1,32,16,64,16]{3,2,4,1,0:T(8,128)(2,1)S(1)} %bitcast.158), kind=kLoop, calls=%fused_computation.87 | loop fusion | flops 6291456 | bytes 8388608
  305.3 9.5 %reshape.545 = bf16[4,2,262144]{2,1,0:T(2,128)(2,1)} reshape(bf16[4,32,16,16,64]{4,3,2,1,0:T(8,128)(2,1)} %fusion.56) | data formatting | bytes 8388608
  314.9 8.4 %all-to-all-start.3 = ((bf16[4,2,262144]{2,1,0:T(2,128)(2,1)}), bf16[4,2,262144]{2,1,0:T(2,128)(2,1)}, u32[]{:S(2)}, u32[]{:S(2)}) async-start(bf16[4,2,262144]{2,1,0:T(2,128)(2,1)} %reshape.545), calls=%async_computation.3 | async-start | bytes 8388608 | tf_op jit(solution)/shard_map/all_to_all | solution.py:102
  323.5 89.3 %all-to-all-done.3 = bf16[4,2,262144]{2,1,0:T(2,128)(2,1)} async-done(((bf16[4,2,262144]{2,1,0:T(2,128)(2,1)}), bf16[4,2,262144]{2,1,0:T(2,128)(2,1)}, u32[]{:S(2)}, u32[]{:S(2)}) %all-to-all-start.3) | async-done | bytes 4194336 | tf_op jit(solution)/shard_map/all_to_all | solution.py:102
  412.8 9.3 %reshape.546 = bf16[4,32,16,16,64]{4,3,2,1,0:T(8,128)(2,1)} reshape(bf16[4,2,262144]{2,1,0:T(2,128)(2,1)} %all-to-all-done.3) | data formatting | bytes 8388608
  422.1 9.9 %bitcast_bitcast_fusion = bf16[32,16,64,4,16]{2,1,4,0,3:T(8,128)(2,1)} fusion(bf16[4,32,16,16,64]{4,3,2,1,0:T(8,128)(2,1)} %reshape.546), kind=kLoop, calls=%fused_computation.86 | loop fusion | bytes 8388608 | tf_op jit(solution)/shard_map/reshape | solution.py:101
  432.0 8.7 %copy.128 = bf16[32,16,64,4,16]{2,4,3,1,0:T(8,128)(2,1)} copy(bf16[32,16,64,4,16]{2,1,4,0,3:T(8,128)(2,1)} %bitcast_bitcast_fusion) | data formatting | bytes 8388608 | tf_op jit(solution)/shard_map/reshape | solution.py:101
  440.7 19.0 %fusion.36 = f32[32,16,64,256]{3,2,1,0:T(8,128)} fusion(bf16[32,16,64,64]{2,3,1,0:T(8,128)(2,1)} %bitcast.147, bf16[64,256,1,1]{1,0,2,3:T(8,128)(2,1)S(1)} %reshape.536), kind=kOutput, calls=%fused_computation.63 | convolution fusion | flops 1073741824 | bytes 37781504 | tf_op jit(solution)/shard_map/dot_general | solution.py:107
  459.7 32.5 %fusion.54 = (f32[]{:T(128)}, f32[]{:T(128)}, f32[32,16,64,256]{3,2,1,0:T(8,128)}) fusion(f32[32,16,64,256]{3,2,1,0:T(8,128)} %fusion.36, bf16[32,16,64,256]{3,2,1,0:T(8,128)(2,1)} %param.3, bf16[64,64]{1,0:T(8,128)(2,1)S(1)} %copy-done), kind=kOutput, calls=%fused_computation.84 | convolution fusion | flops 1174405120 | bytes 83894280 | tf_op jit(solution)/shard_map/yzcx,co->yzox/dot_general | solution.py:111
  492.3 43.2 %all-reduce = (f32[]{:T(128)}, f32[]{:T(128)}) all-reduce(f32[]{:T(128)} %get-tuple-element.6, f32[]{:T(128)} %get-tuple-element.5), channel_id=1, replica_groups=mesh['py'=4,'pz'=8] {'py','pz'}, use_global_device_ids=true, to_apply=%region_3.4 | all-reduce | flops 2 | bytes 16 | tf_op jit(solution)/shard_map/psum | solution.py:114
  538.1 18.5 %multiply_convert_fusion = bf16[32,16,64,256]{3,2,1,0:T(8,128)(2,1)} fusion(f32[32,16,64,256]{3,2,1,0:T(8,128)} %get-tuple-element.29, f32[]{:T(128)S(6)} %rsqrt.3, f32[]{:T(128)S(6)} %div.32), kind=kLoop, calls=%fused_computation.11 | loop fusion | flops 25165824 | bytes 50331656 | tf_op jit(solution)/shard_map/convert_element_type | solution.py:117
  (34 shorter events, 29.4 us)
Async XLA Ops:
  0.0 459.7 %copy-start = (bf16[64,64]{1,0:T(8,128)(2,1)S(1)}, bf16[64,64]{1,0:T(8,128)(2,1)}, u32[]{:S(2)}) copy-start(bf16[64,64]{1,0:T(8,128)(2,1)} %param.5) | copy-start | bytes 24580
  34.0 95.5 %all-to-all-start = ((bf16[4,2,262144]{2,1,0:T(2,128)(2,1)}), bf16[4,2,262144]{2,1,0:T(2,128)(2,1)}, u32[]{:S(2)}, u32[]{:S(2)}) async-start(bf16[4,2,262144]{2,1,0:T(2,128)(2,1)} %reshape.539), calls=%async_computation | async-start | bytes 8388608 | tf_op jit(solution)/shard_map/all_to_all | solution.py:79
  175.7 18.4 %all-to-all-start.1 = ((bf16[8,2,32768]{2,1,0:T(2,128)(2,1)}), bf16[8,2,32768]{2,1,0:T(2,128)(2,1)S(1)}, u32[]{:S(2)}, u32[]{:S(2)}) async-start(bf16[8,2,32768]{2,1,0:T(2,128)(2,1)} %reshape.541), calls=%async_computation.1 | async-start | bytes 2097152 | tf_op jit(solution)/shard_map/all_to_all | solution.py:85
  314.9 97.9 %all-to-all-start.3 = ((bf16[4,2,262144]{2,1,0:T(2,128)(2,1)}), bf16[4,2,262144]{2,1,0:T(2,128)(2,1)}, u32[]{:S(2)}, u32[]{:S(2)}) async-start(bf16[4,2,262144]{2,1,0:T(2,128)(2,1)} %reshape.545), calls=%async_computation.3 | async-start | bytes 8388608 | tf_op jit(solution)/shard_map/all_to_all | solution.py:102
